TPU v7x, 32 devices: a whole 2x2x4 slice. The times are simulated.
32 devices in a mesh: dp: 8 (over z, core), fsdp: 4 (over y, x).
Axes of the slice: x: 2, y: 2, z: 4, core: 2. Of those that a mesh axis runs over, the one named last changes fastest.
Arguments:
- logits: bfloat16 [4096, 32000], P('dp', 'fsdp'), may hold values from -115 to 125
- labels: int32 [4096], P('dp'), may hold values from 0 to 31999
- activations: bfloat16 [4096, 5120], P('dp', 'fsdp'), may hold values from -6 to 6
- proj_in: bfloat16 [5120, 64], P('fsdp'), may hold values from -0.078125 to 0.078125
- proj_out: bfloat16 [32000, 64], P('fsdp'), may hold values from -6 to 6
Outputs:
- features: float32 [512, 4096], P(('dp', 'fsdp'))
- gram: float32 [4096, 4096], P('fsdp', 'dp')
All inputs are finite; a program needn't handle non-finite values.
Results may differ from a plain program's by a relative error of at most 0.014.
Values may be sent and summed in bfloat16 or wider, within the bound.
No kernel may reach another device: no remote copies, remote signals or barrier semaphores. Data moves between devices by JAX's collectives and lax.ppermute only.
A program may use at most 64 MiB of HBM per device.

v0:
```python
import jax
import jax.numpy as jnp
from jax import lax
from jax.sharding import PartitionSpec as P

SEQ = 8


def body(logits, labels, activations, proj_in, proj_out):
    vocab_local = logits.shape[1]
    values = logits.astype(jnp.float32)
    local_top = jnp.max(values, axis=1)
    row_top = lax.pmax(local_top, "fsdp")
    row_sum = lax.psum(jnp.sum(jnp.exp(values - row_top[:, None]), axis=1), "fsdp")
    prob = jnp.exp(values - row_top[:, None]) / row_sum[:, None]
    columns = lax.axis_index("fsdp") * vocab_local + lax.broadcasted_iota(
        jnp.int32, (1, vocab_local), 1
    )
    onehot = (columns == labels[:, None]).astype(jnp.float32)
    errors = (prob - onehot).astype(jnp.bfloat16)
    part_left = jnp.dot(activations, proj_in, preferred_element_type=jnp.float32)
    part_right = jnp.dot(errors, proj_out, preferred_element_type=jnp.float32)
    left, right = (
        lax.psum_scatter(part_left, "fsdp", scatter_dimension=0, tiled=True),
        lax.psum_scatter(part_right, "fsdp", scatter_dimension=0, tiled=True),
    )
    count = left.shape[0] // SEQ
    width_in = proj_in.shape[1]
    width_out = proj_out.shape[1]
    sketch = jnp.einsum(
        "esi,esj->eij", left.reshape(count, SEQ, width_in), right.reshape(count, SEQ, width_out)
    )
    features = sketch.reshape(count, width_in * width_out)
    rounded = features.astype(jnp.bfloat16)
    feat_all = features.shape[1]
    gram_rows = feat_all // lax.axis_size("fsdp")
    row_start = lax.axis_index("fsdp") * gram_rows
    folded = lax.all_gather(rounded, "fsdp", axis=0, tiled=True)
    column_share = lax.all_to_all(folded, "dp", split_axis=1, concat_axis=0, tiled=True)
    row_share = lax.dynamic_slice_in_dim(folded, row_start, gram_rows, 1)
    gram = lax.dot_general(
        lax.all_gather(row_share, "dp", axis=0, tiled=True),
        column_share,
        (((0,), (0,)), ((), ())),
        preferred_element_type=jnp.float32,
    )
    return (features, gram)


def solution(mesh):
    in_specs = (P("dp", "fsdp"), P("dp"), P("dp", "fsdp"), P("fsdp", None), P("fsdp", None))
    out_specs = (P(("dp", "fsdp"), None), P("fsdp", "dp"))
    return jax.shard_map(body, mesh=mesh, in_specs=in_specs, out_specs=out_specs, check_vma=False)
```

profile of v0, /device:TPU:0, one launch (start us, length us, event | category | flops | bytes accessed | tf_op | source)
XLA Modules:
  0.0 152.0 jit_solution(3357230668672112707)
XLA Ops:
  7.2 0.0 copy-start
  7.2 0.0 reduce-scatter.5.cloned.1.call-start
  7.2 4.6 %reduce_max.14 = bf16[512]{0:T(512)(128)(2,1)S(1)} reduce(bf16[512,8000]{0,1:T(8,128)(2,1)} %param.5, bf16[]{:T(256)} %constant.7.clone.1), dimensions={1}, to_apply=%region_1.0 | reduce | flops 4095488 | bytes 8193026 | tf_op jit(solution)/shard_map/reduce_max | solution.py:12
  11.9 11.4 %pmax.7 = f32[512]{0:T(512)S(1)} all-reduce(bf16[512]{0:T(512)(128)(2,1)S(1)} %reduce_max.14), channel_id=1, replica_groups=mesh['dp'=8,'fsdp'=4] {'fsdp'}, use_global_device_ids=true, to_apply=%region_2.0 | all-reduce | flops 512 | bytes 3072 | tf_op jit(solution)/shard_map/pmax | solution.py:13
  23.2 6.1 %fusion = f32[512]{0:T(512)S(1)} fusion(bf16[512,8000]{0,1:T(8,128)(2,1)} %param.5, f32[512]{0:T(512)S(1)} %pmax.7), kind=kLoop, calls=%fused_computation.2 | loop fusion | flops 12287488 | bytes 8196096 | tf_op jit(solution)/shard_map/reduce_sum | solution.py:14
  29.3 8.0 %psum.7 = f32[512]{0:T(512)S(1)} all-reduce(f32[512]{0:T(512)S(1)} %fusion), channel_id=1, replica_groups=mesh['dp'=8,'fsdp'=4] {'fsdp'}, use_global_device_ids=true, to_apply=%region_4.0 | all-reduce | flops 512 | bytes 4096 | tf_op jit(solution)/shard_map/psum | solution.py:14
  37.3 10.7 %fusion.1 = f32[512,64]{0,1:T(8,128)} fusion(bf16[8000,64]{0,1:T(8,128)(2,1)S(1)} %copy-done.3, bf16[512,8000]{0,1:T(8,128)(2,1)} %param.5, s32[512]{0:T(512)S(1)} %copy-done.4, f32[512]{0:T(512)S(1)} %psum.7, f32[512]{0:T(512)S(1)} %pmax.7, s32[8000]{0:T(1024)S(1)} %iota_add_fusion), kind=kOutput, calls=%fused_computation.3 | convolution fusion | flops 552960000 | bytes 9385216 | tf_op jit(solution)/shard_map/dot_general | solution.py:22
  48.0 0.0 reduce-scatter.5.cloned.1.call-update
  48.0 0.0 reduce-scatter.3.cloned.1.call-start
  48.1 1.2 fusion.5
  49.3 0.0 reduce-scatter.3.cloned.1.call-update
  49.3 0.0 all-gather.2.cloned.1.call-start
  49.3 23.3 %reduce-scatter.5.cloned.1.call-done = f32[128,64]{0,1:T(8,128)} async-done(((f32[512,64]{0,1:T(8,128)}), f32[128,64]{0,1:T(8,128)}) %reduce-scatter.5.cloned.1.call-update) | async-done | bytes 32784 | tf_op jit(solution)/shard_map/reduce_scatter | solution.py:25
  72.6 0.9 copy.15
  73.5 26.6 %reduce-scatter.3.cloned.1.call-done = f32[128,64]{0,1:T(8,128)} async-done(((f32[512,64]{0,1:T(8,128)}), f32[128,64]{0,1:T(8,128)}) %reduce-scatter.3.cloned.1.call-update) | async-done | bytes 32784 | tf_op jit(solution)/shard_map/reduce_scatter | solution.py:24
  100.1 0.9 copy.14
  101.0 0.3 fusion.2
  101.3 0.2 reshape.26
  101.5 10.5 %all_gather.6 = bf16[64,4096]{1,0:T(8,128)(2,1)S(1)} all-gather(bf16[16,4096]{1,0:T(8,128)(2,1)S(1)} %convert_element_type.15), channel_id=1, replica_groups=mesh['dp'=8,'fsdp'=4] {'fsdp'}, dimensions={0}, use_global_device_ids=true | all-gather | bytes 655360 | tf_op jit(solution)/shard_map/all_gather | solution.py:38
  112.0 0.7 constant_dynamic-slice_fusion
  112.6 0.0 all-gather.2.cloned.1.call-update
  112.7 28.1 %all_to_all.19 = bf16[64,8,512]{2,0,1:T(8,128)(2,1)S(1)} all-to-all(bf16[64,8,512]{2,0,1:T(8,128)(2,1)S(1)} %bitcast.20), channel_id=1, replica_groups=mesh['dp'=8,'fsdp'=4] {'dp'}, dimensions={1} | all-to-all | bytes 1048576 | tf_op jit(solution)/shard_map/all_to_all | solution.py:39
  140.9 1.4 all-gather.2.cloned.1.call-done
  142.2 3.3 %fusion.6 = f32[1024,512]{1,0:T(8,128)} fusion(bf16[512,1024]{1,0:T(8,128)(2,1)} %all-gather.2.cloned.1.call-done, bf16[512,512]{1,0:T(8,128)(2,1)S(1)} %bitcast.19), kind=kOutput, calls=%fused_computation.11 | convolution fusion | flops 536870912 | bytes 3670016 | tf_op jit(solution)/shard_map/dot_general | solution.py:41
  (12 shorter events, 0.1 us)
Async XLA Ops:
  7.2 40.9 %copy-start = (bf16[512,1280]{1,0:T(8,128)(2,1)S(1)}, bf16[512,1280]{1,0:T(8,128)(2,1)}, u32[]{:S(2)}) copy-start(bf16[512,1280]{1,0:T(8,128)(2,1)} %param.7) | copy-start | bytes 3932164
  7.2 65.4 %reduce-scatter.5.cloned.1.call-start = ((), (), s32[]{:S(2)}) async-start(), calls=%async_computation.4 | async-start | bytes 163840 | tf_op jit(solution)/shard_map/reduce_scatter | solution.py:25
  7.2 30.1 %copy-start.3 = (bf16[8000,64]{0,1:T(8,128)(2,1)S(1)}, bf16[8000,64]{0,1:T(8,128)(2,1)}, u32[]{:S(2)}) copy-start(bf16[8000,64]{0,1:T(8,128)(2,1)} %param.9) | copy-start | bytes 3072004
  7.2 30.1 %copy-start.4 = (s32[512]{0:T(512)S(1)}, s32[512]{0:T(512)}, u32[]{:S(2)}) copy-start(s32[512]{0:T(512)} %param.6) | copy-start | bytes 6148
  37.3 10.8 %copy-start.2 = (bf16[1280,64]{0,1:T(8,128)(2,1)S(1)}, bf16[1280,64]{0,1:T(8,128)(2,1)}, u32[]{:S(2)}) copy-start(bf16[1280,64]{0,1:T(8,128)(2,1)} %param.8) | copy-start | bytes 491524
  48.0 52.1 %reduce-scatter.3.cloned.1.call-start = ((), (), s32[]{:S(2)}) async-start(), calls=%async_computation.3 | async-start | bytes 163840 | tf_op jit(solution)/shard_map/reduce_scatter | solution.py:24
  49.3 92.9 %all-gather.2.cloned.1.call-start = ((), (), s32[]{:S(2)}) async-start(), calls=%async_computation.5 | async-start | bytes 1179648 | tf_op jit(solution)/shard_map/all_gather | solution.py:42
  101.5 44.0 %copy-start.1 = (f32[16,4096]{1,0:T(8,128)}, f32[16,4096]{1,0:T(8,128)S(1)}, u32[]{:S(2)}) copy-start(f32[16,4096]{1,0:T(8,128)S(1)} %reshape.26) | copy-start | bytes 786436
Sparse Core Ops, SparseCore 0:
  48.1 24.4 reduce-scatter.4
  75.9 24.1 reduce-scatter.2
  112.8 29.3 all-gather.1
where the time goes:
time: 153 us; the launch traced here: 152 us
  blocking collectives  58 us (38%)
  waiting for transfers between devices  51.3 us (34%)
  matrix products  15.4 us (10%)
  between operations  13.8 us (9%)
  other arithmetic  10.7 us (7%)
  local copies, waits for them, and re-layouts  2.64 us (2%)
    all_to_all x1, blocking collectives, body(): lax.all_to_all(folded, 'dp', split_axis=1, concat_axis=0, tiled=True)  28.1 us
    reduce_scatter x1, waiting for transfers between devices, body(): lax.psum_scatter(part_left, 'fsdp', scatter_dimension=0, tiled=True)  26.6 us
    reduce_scatter x1, waiting for transfers between devices, body(): lax.psum_scatter(part_right, 'fsdp', scatter_dimension=0, tiled=True)  23.3 us
    pmax x1, blocking collectives, body(): row_top = lax.pmax(local_top, 'fsdp')  11.4 us
    dot_general x1, matrix products, body(): part_right = jnp.dot(errors, proj_out, preferred_element_type=jnp.float32)  10.7 us
    all_gather x1, blocking collectives, body(): folded = lax.all_gather(rounded, 'fsdp', axis=0, tiled=True)  10.5 us
    psum x1, blocking collectives, body(): lax.psum(jnp.sum(jnp.exp(values - row_top[:, None]), axis=1), 'fsdp')  7.98 us
    reduce_sum x1, other arithmetic, body(): jnp.sum(jnp.exp(values - row_top[:, None]), axis=1)  6.09 us
  transfers between devices with their start and end apart: 3, of which 3 were waited for; matrix products, arithmetic and copies ran while one was open for 1% of the time, Pallas kernels for 0%

commit v1 on v0

--- a/solution.py
+++ b/solution.py
@@ -35,7 +35,12 @@
     feat_all = features.shape[1]
     gram_rows = feat_all // lax.axis_size("fsdp")
     row_start = lax.axis_index("fsdp") * gram_rows
-    folded = lax.all_gather(rounded, "fsdp", axis=0, tiled=True)
+    ring = [rounded]
+    for hop in range(3):
+        ring.append(lax.ppermute(ring[-1], "fsdp", [(dev, (dev + 1) % 4) for dev in range(4)]))
+    folded = jnp.roll(
+        jnp.concatenate(ring[::-1], axis=0), (lax.axis_index("fsdp") + 1) * ring[0].shape[0], axis=0
+    )
     column_share = lax.all_to_all(folded, "dp", split_axis=1, concat_axis=0, tiled=True)
     row_share = lax.dynamic_slice_in_dim(folded, row_start, gram_rows, 1)
     gram = lax.dot_general(

time: 153 us -> 160 us (1.046)
  waiting for transfers between devices: 51.3 us -> 66.8 us
  blocking collectives: 58 us -> 47.5 us
  starting transfers between devices: 0.12 us -> 2.24 us
    ppermute x0 -> x3, waiting for transfers between devices: none -> 15.5 us  [body(): lax.ppermute(ring[-1], 'fsdp', [(dev, (dev + 1) % 4) for dev in range(4)])]
    all_gather x1 -> x0, blocking collectives: 10.5 us -> none  [body(): folded = lax.all_gather(rounded, 'fsdp', axis=0, tiled=True)]
    ppermute x0 -> x3, starting transfers between devices: none -> 2.12 us  [body(): lax.ppermute(ring[-1], 'fsdp', [(dev, (dev + 1) % 4) for dev in range(4)])]
  transfers between devices with their start and end apart: 3 -> 6, of which waited for: 3 -> 6; matrix products, arithmetic and copies ran while one was open for 1% -> 1% of each run, Pallas kernels for 0% -> 0%
where the time goes in v1:
time: 160 us
  waiting for transfers between devices  66.8 us (42%)
  blocking collectives  47.5 us (30%)
  matrix products  15.4 us (10%)
  between operations  13.9 us (9%)
  other arithmetic  10.7 us (7%)
  local copies, waits for them, and re-layouts  2.87 us (2%)
  starting transfers between devices  2.24 us (1%)
    all_to_all x1, blocking collectives, body(): lax.all_to_all(folded, 'dp', split_axis=1, concat_axis=0, tiled=True)  28.2 us
    reduce_scatter x1, waiting for transfers between devices, body(): lax.psum_scatter(part_left, 'fsdp', scatter_dimension=0, tiled=True)  26.6 us
    reduce_scatter x1, waiting for transfers between devices, body(): lax.psum_scatter(part_right, 'fsdp', scatter_dimension=0, tiled=True)  23.3 us
    ppermute x3, waiting for transfers between devices, body(): lax.ppermute(ring[-1], 'fsdp', [(dev, (dev + 1) % 4) for dev in range(4)])  15.5 us
    pmax x1, blocking collectives, body(): row_top = lax.pmax(local_top, 'fsdp')  11.4 us
    dot_general x1, matrix products, body(): part_right = jnp.dot(errors, proj_out, preferred_element_type=jnp.float32)  10.7 us
    psum x1, blocking collectives, body(): lax.psum(jnp.sum(jnp.exp(values - row_top[:, None]), axis=1), 'fsdp')  7.98 us
    reduce_sum x1, other arithmetic, body(): jnp.sum(jnp.exp(values - row_top[:, None]), axis=1)  6.09 us
  transfers between devices with their start and end apart: 6, of which 6 were waited for; matrix products, arithmetic and copies ran while one was open for 1% of the time, Pallas kernels for 0%

profile of v1, /device:TPU:0, one launch (start us, length us, event | category | flops | bytes accessed | tf_op | source)
XLA Modules:
  0.0 159.5 jit_solution(1890970716217967239)
XLA Ops:
  7.2 0.0 reduce-scatter.5.cloned.1.call-start
  7.2 4.6 %reduce_max.14 = bf16[512]{0:T(512)(128)(2,1)S(1)} reduce(bf16[512,8000]{0,1:T(8,128)(2,1)} %param.5, bf16[]{:T(256)} %constant.40.clone.1), dimensions={1}, to_apply=%region_1.0 | reduce | flops 4095488 | bytes 8193026 | tf_op jit(solution)/shard_map/reduce_max | solution.py:12
  11.9 11.4 %pmax.7 = f32[512]{0:T(512)S(1)} all-reduce(bf16[512]{0:T(512)(128)(2,1)S(1)} %reduce_max.14), channel_id=1, replica_groups=mesh['dp'=8,'fsdp'=4] {'fsdp'}, use_global_device_ids=true, to_apply=%region_2.0 | all-reduce | flops 512 | bytes 3072 | tf_op jit(solution)/shard_map/pmax | solution.py:13
  23.2 6.1 %fusion = f32[512]{0:T(512)S(1)} fusion(bf16[512,8000]{0,1:T(8,128)(2,1)} %param.5, f32[512]{0:T(512)S(1)} %pmax.7), kind=kLoop, calls=%fused_computation.2 | loop fusion | flops 12287488 | bytes 8196096 | tf_op jit(solution)/shard_map/reduce_sum | solution.py:14
  29.3 8.0 %psum.7 = f32[512]{0:T(512)S(1)} all-reduce(f32[512]{0:T(512)S(1)} %fusion), channel_id=1, replica_groups=mesh['dp'=8,'fsdp'=4] {'fsdp'}, use_global_device_ids=true, to_apply=%region_4.0 | all-reduce | flops 512 | bytes 4096 | tf_op jit(solution)/shard_map/psum | solution.py:14
  37.3 10.7 %fusion.1 = f32[512,64]{0,1:T(8,128)} fusion(bf16[8000,64]{0,1:T(8,128)(2,1)S(1)} %copy-done.3, bf16[512,8000]{0,1:T(8,128)(2,1)} %param.5, s32[512]{0:T(512)S(1)} %copy-done.4, f32[512]{0:T(512)S(1)} %psum.7, f32[512]{0:T(512)S(1)} %pmax.7, s32[8000]{0:T(1024)S(1)} %iota_add_fusion), kind=kOutput, calls=%fused_computation.3 | convolution fusion | flops 552960000 | bytes 9385216 | tf_op jit(solution)/shard_map/dot_general | solution.py:22
  48.0 0.0 reduce-scatter.3.cloned.1.call-start
  48.1 1.2 fusion.5
  49.3 0.0 all-gather.2.cloned.1.call-start
  49.3 23.3 %reduce-scatter.5.cloned.1.call-done = f32[128,64]{0,1:T(8,128)} async-done(((f32[512,64]{0,1:T(8,128)}), f32[128,64]{0,1:T(8,128)}) %reduce-scatter.5.cloned.1.call-update) | async-done | bytes 32784 | tf_op jit(solution)/shard_map/reduce_scatter | solution.py:25
  72.6 0.9 copy.15
  73.5 26.6 %reduce-scatter.3.cloned.1.call-done = f32[128,64]{0,1:T(8,128)} async-done(((f32[512,64]{0,1:T(8,128)}), f32[128,64]{0,1:T(8,128)}) %reduce-scatter.3.cloned.1.call-update) | async-done | bytes 32784 | tf_op jit(solution)/shard_map/reduce_scatter | solution.py:24
  100.1 0.9 copy.14
  101.0 0.3 fusion.2
  101.3 0.2 reshape.26
  101.5 1.5 collective-permute-start
  103.0 4.4 %collective-permute-done = bf16[16,4096]{1,0:T(8,128)(2,1)S(1)} collective-permute-done((bf16[16,4096]{1,0:T(8,128)(2,1)S(1)}, bf16[16,4096]{1,0:T(8,128)(2,1)S(1)}, u32[]{:S(2)}, u32[]{:S(2)}) %collective-permute-start) | collective-permute-done | bytes 131104 | tf_op jit(solution)/shard_map/ppermute | solution.py:40
  107.4 0.6 collective-permute-start.1
  108.0 5.3 %collective-permute-done.1 = bf16[16,4096]{1,0:T(8,128)(2,1)S(1)} collective-permute-done((bf16[16,4096]{1,0:T(8,128)(2,1)S(1)}, bf16[16,4096]{1,0:T(8,128)(2,1)S(1)}, u32[]{:S(2)}, u32[]{:S(2)}) %collective-permute-start.1) | collective-permute-done | bytes 131104 | tf_op jit(solution)/shard_map/ppermute | solution.py:40
  113.3 5.9 %collective-permute-done.2 = bf16[16,4096]{1,0:T(8,128)(2,1)S(1)} collective-permute-done((bf16[16,4096]{1,0:T(8,128)(2,1)S(1)}, bf16[16,4096]{1,0:T(8,128)(2,1)S(1)}, u32[]{:S(2)}, u32[]{:S(2)}) %collective-permute-start.2) | collective-permute-done | bytes 131104 | tf_op jit(solution)/shard_map/ppermute | solution.py:40
  119.3 0.8 dynamic_slice.7
  120.2 28.2 %all_to_all.19 = bf16[64,8,512]{2,0,1:T(8,128)(2,1)S(1)} all-to-all(bf16[64,8,512]{2,0,1:T(8,128)(2,1)S(1)} %bitcast.20), channel_id=1, replica_groups=mesh['dp'=8,'fsdp'=4] {'dp'}, dimensions={1} | all-to-all | bytes 1048576 | tf_op jit(solution)/shard_map/all_to_all | solution.py:44
  148.4 1.4 all-gather.2.cloned.1.call-done
  149.7 3.3 %fusion.6 = f32[1024,512]{1,0:T(8,128)} fusion(bf16[512,1024]{1,0:T(8,128)(2,1)} %all-gather.2.cloned.1.call-done, bf16[512,512]{1,0:T(8,128)(2,1)S(1)} %bitcast.18), kind=kOutput, calls=%fused_computation.19 | convolution fusion | flops 536870912 | bytes 3670016 | tf_op jit(solution)/shard_map/dot_general | solution.py:46
  (26 shorter events, 0.3 us)
Async XLA Ops:
  7.2 40.9 %copy-start = (bf16[512,1280]{1,0:T(8,128)(2,1)S(1)}, bf16[512,1280]{1,0:T(8,128)(2,1)}, u32[]{:S(2)}) copy-start(bf16[512,1280]{1,0:T(8,128)(2,1)} %param.7) | copy-start | bytes 3932164
  7.2 65.4 %reduce-scatter.5.cloned.1.call-start = ((), (), s32[]{:S(2)}) async-start(), calls=%async_computation.4 | async-start | bytes 163840 | tf_op jit(solution)/shard_map/reduce_scatter | solution.py:25
  7.2 30.1 %copy-start.3 = (bf16[8000,64]{0,1:T(8,128)(2,1)S(1)}, bf16[8000,64]{0,1:T(8,128)(2,1)}, u32[]{:S(2)}) copy-start(bf16[8000,64]{0,1:T(8,128)(2,1)} %param.9) | copy-start | bytes 3072004
  7.2 30.1 %copy-start.4 = (s32[512]{0:T(512)S(1)}, s32[512]{0:T(512)}, u32[]{:S(2)}) copy-start(s32[512]{0:T(512)} %param.6) | copy-start | bytes 6148
  37.3 10.8 %copy-start.2 = (bf16[1280,64]{0,1:T(8,128)(2,1)S(1)}, bf16[1280,64]{0,1:T(8,128)(2,1)}, u32[]{:S(2)}) copy-start(bf16[1280,64]{0,1:T(8,128)(2,1)} %param.8) | copy-start | bytes 491524
  48.0 52.1 %reduce-scatter.3.cloned.1.call-start = ((), (), s32[]{:S(2)}) async-start(), calls=%async_computation.3 | async-start | bytes 163840 | tf_op jit(solution)/shard_map/reduce_scatter | solution.py:24
  49.3 100.4 %all-gather.2.cloned.1.call-start = ((), (), s32[]{:S(2)}) async-start(), calls=%async_computation.5 | async-start | bytes 1179648 | tf_op jit(solution)/shard_map/all_gather | solution.py:47
  101.5 51.5 %copy-start.1 = (f32[16,4096]{1,0:T(8,128)}, f32[16,4096]{1,0:T(8,128)S(1)}, u32[]{:S(2)}) copy-start(f32[16,4096]{1,0:T(8,128)S(1)} %reshape.26) | copy-start | bytes 786436
  101.5 5.9 %collective-permute-start = (bf16[16,4096]{1,0:T(8,128)(2,1)S(1)}, bf16[16,4096]{1,0:T(8,128)(2,1)S(1)}, u32[]{:S(2)}, u32[]{:S(2)}) collective-permute-start(bf16[16,4096]{1,0:T(8,128)(2,1)S(1)} %convert_element_type.15), channel_id=1, source_target_pairs={{0,1},{1,2},{2,3},{3,0},{4,5},{5,6},{6,7},{7,4},{8,9},{9,10},{10,1... | collective-permute-start | bytes 393224 | tf_op jit(solution)/shard_map/ppermute | solution.py:40
  107.4 5.9 %collective-permute-start.1 = (bf16[16,4096]{1,0:T(8,128)(2,1)S(1)}, bf16[16,4096]{1,0:T(8,128)(2,1)S(1)}, u32[]{:S(2)}, u32[]{:S(2)}) collective-permute-start(bf16[16,4096]{1,0:T(8,128)(2,1)S(1)} %collective-permute-done), channel_id=1, source_target_pairs={{0,1},{1,2},{2,3},{3,0},{4,5},{5,6},{6,7},{7,4},{8,9},{9,10},{10,1... | collective-permute-start | bytes 393224 | tf_op jit(solution)/shard_map/ppermute | solution.py:40
  113.3 5.9 %collective-permute-start.2 = (bf16[16,4096]{1,0:T(8,128)(2,1)S(1)}, bf16[16,4096]{1,0:T(8,128)(2,1)S(1)}, u32[]{:S(2)}, u32[]{:S(2)}) collective-permute-start(bf16[16,4096]{1,0:T(8,128)(2,1)S(1)} %collective-permute-done.1), channel_id=1, source_target_pairs={{0,1},{1,2},{2,3},{3,0},{4,5},{5,6},{6,7},{7,4},{8,9},{9,10},{10,1... | collective-permute-start | bytes 393224 | tf_op jit(solution)/shard_map/ppermute | solution.py:40
Sparse Core Ops, SparseCore 0:
  48.1 24.4 reduce-scatter.4
  75.9 24.1 reduce-scatter.2
  120.2 29.4 all-gather.1
